TPU v7x, 32 devices: a whole 2x2x4 slice. The times are simulated.
32 devices in a mesh: rack: 4 (over x, core), chip: 8 (over z, y).
Axes of the slice: x: 2, y: 2, z: 4, core: 2. Of those that a mesh axis runs over, the one named last changes fastest.
Arguments:
- points: float32 [64, 4, 32, 256], P(('rack', 'chip')), may hold values from -6 to 6
- counts: int32 [64, 256], P(('rack', 'chip')), may hold values from 1 to 32
- cells: int32 [64, 256], P(('rack', 'chip')), may hold values from 0 to 2047, as said below
- pfn_weight: float32 [9, 64], replicated, may hold values from -2 to 2
- pfn_gain: float32 [64], replicated, may hold values from 0.5 to 1.5
- pfn_bias: float32 [64], replicated, may hold values from -3 to 3
- conv_weight: float32 [4, 9, 4096], replicated, may hold values from -0.25 to 0.25
- bn_gain: float32 [4, 64], replicated, may hold values from 0.5 to 1.5
- bn_bias: float32 [4, 64], replicated, may hold values from -3 to 3
- cotangent: float32 [64, 64, 4, 128], P(('rack', 'chip')), may hold values from -0.006 to 0.006
Outputs:
- features: float32 [64, 64, 4, 128], P(('rack', 'chip'))
- conv_grads: float32 [4, 9, 4096], replicated
- norm_grads: float32 [2, 4, 64], replicated
- pillar_grad: float32 [64, 64, 256], P(('rack', 'chip'))
Inputs may be any that keep to these rules, and one draw needn't show every extreme that they name: `cells`: within one sweep no two pillars share a cell.
All inputs are finite; a program needn't handle non-finite values.
Results may differ from a plain program's by a relative error of at most 0.0003.
Values sent between devices are 32-bit elements; how exact they have to be, the bound alone decides.
A program may use at most 128 MiB of HBM per device.

v0:
```python
import functools

import jax
import jax.numpy as jnp
from jax import lax
from jax.experimental import pallas as pl
from jax.experimental.pallas import tpu as pltpu
from jax.sharding import PartitionSpec as P

LAYERS = 4
EPS = 1e-05
F32 = jnp.float32
BF16 = jnp.bfloat16
NN = (((1,), (0,)), ((), ()))
NT = (((1,), (1,)), ((), ()))
LOWEST = -3e38


def dot(a, b, dims=NN):
    return lax.dot_general(a, b, dims, preferred_element_type=F32)


def split(x):
    hi = x.astype(BF16)
    lo = (x - hi.astype(F32)).astype(BF16)
    return hi, lo


def kernel(
    dims,
    points,
    counts,
    cells,
    pw_s,
    pw_t,
    pfn_gb,
    wf,
    wb,
    wb0,
    bn_cols,
    cot,
    feat,
    grads,
    norms,
    pgrad,
    xs,
    gs,
    wfs,
    wbs,
    wb0s,
    onehot,
    bm,
    mx,
    sq,
    xh,
    yy,
    gz_s,
    st0,
    st,
    rs,
    rbuf,
    st_send,
    st_recv,
    rs_send,
    rs_recv,
    ag_send,
    ag_recv,
):
    n_rack, n_chip, sweeps, maxp, gh, gw, pill, ch, owners = dims
    n = n_rack * n_chip
    h2, w2 = gh // 2, gw // 2
    plane = h2 * w2
    pix = sweeps * plane
    rows_per = ch // owners
    kdim = 9 * ch
    me = lax.axis_index("rack") * n_chip + lax.axis_index("chip")

    def device(t):
        return {"rack": lax.div(t, n_chip), "chip": lax.rem(t, n_chip)}

    def peers(body):
        def step(k, carry):
            body(lax.rem(me + k, n))
            return carry

        lax.fori_loop(1, n, step, 0)

    barrier = pltpu.get_barrier_semaphore()
    peers(
        lambda t: pl.semaphore_signal(
            barrier, inc=1, device_id=device(t), device_id_type=pl.DeviceIdType.MESH
        )
    )

    def send_row(buf, rnd, row):
        buf[rnd, me] = row

        def go(t):
            pltpu.make_async_remote_copy(
                src_ref=buf.at[rnd, me],
                dst_ref=buf.at[rnd, me],
                send_sem=st_send.at[rnd],
                recv_sem=st_recv.at[rnd],
                device_id=device(t),
                device_id_type=pl.DeviceIdType.MESH,
            ).start()

        peers(go)

    def wait_row(buf, rnd):
        most = buf.at[rnd, pl.ds(0, n - 1)]
        pltpu.make_async_copy(most, most, st_recv.at[rnd]).wait()
        return buf[rnd]

    def send_parts(layer):
        def go(t):
            def copy():
                pltpu.make_async_remote_copy(
                    src_ref=rs.at[layer, t],
                    dst_ref=rbuf.at[layer, me],
                    send_sem=rs_send.at[layer],
                    recv_sem=rs_recv.at[layer],
                    device_id=device(t),
                    device_id_type=pl.DeviceIdType.MESH,
                ).start()

            if owners == n:
                copy()
            else:
                pl.when(t < owners)(copy)

        peers(go)

    def when_owner(body):
        if owners == n:
            body()
        else:
            pl.when(me < owners)(body)

    def add_parts(layer):
        def body():
            most = rbuf.at[layer, pl.ds(0, n - 1)]
            pltpu.make_async_copy(most, most, rs_recv.at[layer]).wait()
            rbuf[layer, me] = rs[layer, me]
            grads[layer, me] = jnp.sum(rbuf[layer], axis=0)

            def go(t):
                pltpu.make_async_remote_copy(
                    src_ref=grads.at[layer, me],
                    dst_ref=grads.at[layer, me],
                    send_sem=ag_send.at[layer],
                    recv_sem=ag_recv.at[layer],
                    device_id=device(t),
                    device_id_type=pl.DeviceIdType.MESH,
                ).start()

            peers(go)

        when_owner(body)

    slot = lax.broadcasted_iota(jnp.int32, (maxp, pill), 0)
    lane = lax.broadcasted_iota(jnp.int32, (1, 2 * ch), 1)
    per_sweep = []
    totals = [jnp.zeros((1, 1), F32)] * 9
    n_loc = jnp.zeros((1, 1), F32)
    for s in range(sweeps):
        valid = slot < counts[s : s + 1, :]
        mask = valid.astype(F32)
        cnt = counts[s : s + 1, :].astype(F32)
        sums = [jnp.sum(points[s, f] * mask, axis=0, keepdims=True) for f in range(4)]
        cents = [sums[f] / cnt for f in range(3)]
        cell = cells[s : s + 1, :]
        row = lax.shift_right_logical(cell, gw.bit_length() - 1)
        col = cell & (gw - 1)
        col_pos = col.astype(F32) * (2.0 / gw) - 1.0
        row_pos = row.astype(F32) * (2.0 / gh) - 1.0
        feats = sums + [sums[f] - cnt * cents[f] for f in range(3)]
        feats += [sums[0] - cnt * col_pos, sums[1] - cnt * row_pos]
        totals = [t + jnp.sum(f, axis=1, keepdims=True) for t, f in zip(totals, feats)]
        n_loc = n_loc + jnp.sum(cnt, axis=1, keepdims=True)
        per_sweep.append(cents + [col_pos, row_pos])
        spot = ((row & 1) * 2 + (col & 1)) * plane
        spot = spot + lax.shift_right_logical(row, 1) * w2 + lax.shift_right_logical(col, 1)
        for k in range(4):
            ids = lax.broadcasted_iota(jnp.int32, (plane, pill), 0) + k * plane
            onehot[s, k * plane : (k + 1) * plane, :] = (ids == spot).astype(F32).astype(BF16)
    pw_cols = pw_t[...]
    m_loc = jnp.zeros((ch, 1), F32)
    for f in range(9):
        m_loc = m_loc + pw_cols[:, f : f + 1] * totals[f]
    m_loc = m_loc / n_loc
    for s in range(sweeps):
        base = -m_loc
        for f in range(5):
            base = base - pw_cols[:, f + 4 : f + 5] * per_sweep[s][f]
        bm[s] = base

    def one_channel(c, carry):
        wx = pw_s[0, c] + pw_s[4, c] + pw_s[7, c]
        wy = pw_s[1, c] + pw_s[5, c] + pw_s[8, c]
        wz = pw_s[2, c] + pw_s[6, c]
        wr = pw_s[3, c]
        total = jnp.zeros((8, pill), F32)
        for s in range(sweeps):
            most = jnp.full((8, pill), LOWEST, F32)
            shift = bm[s, pl.ds(c, 1), :]
            have = counts[s : s + 1, :]
            for k in range(maxp // 8):
                part = pl.ds(8 * k, 8)
                ids = lax.broadcasted_iota(jnp.int32, (8, pill), 0) + 8 * k
                ok = ids < have
                h = points[s, 0, part, :] * wx + points[s, 1, part, :] * wy
                h = h + points[s, 2, part, :] * wz + points[s, 3, part, :] * wr + shift
                most = jnp.maximum(most, jnp.where(ok, h, LOWEST))
                h = jnp.where(ok, h, 0.0)
                total = total + h * h
            mx[s, c] = most
        folded = total[:, 0:128]
        for t in range(1, pill // 128):
            folded = folded + total[:, t * 128 : (t + 1) * 128]
        sq[c] = folded
        return carry

    lax.fori_loop(0, ch, one_channel, 0)
    both = jnp.concatenate([jnp.broadcast_to(m_loc, (ch, 128)), jnp.sum(sq[...], axis=1)], axis=0)
    turned = both.T
    row = jnp.where(lane < ch, turned[0:1, :], jnp.sum(turned, axis=0, keepdims=True))
    row = jnp.concatenate([row, jnp.broadcast_to(n_loc, (1, 2 * ch))], axis=1)

    pl.semaphore_wait(barrier, n - 1)
    send_row(st0, 0, row)

    for layer in range(LAYERS):
        hi, lo = split(wf[layer])
        wfs[layer, 0:ch, :] = hi
        wfs[layer, ch : 2 * ch, :] = lo
    for layer in range(LAYERS - 1):
        hi, lo = split(wb[layer])
        wbs[layer, 0:ch, :] = hi
        wbs[layer, ch : 2 * ch, :] = lo
    hi, lo = split(wb0[...])
    wb0s[0 : 4 * ch, :] = hi
    wb0s[4 * ch : 8 * ch, :] = lo

    def columns(row):
        turned = jnp.broadcast_to(row, (8, 2 * ch)).T
        return turned[0:ch, 0:1], turned[ch : 2 * ch, 0:1]

    got = wait_row(st0, 0)
    n_all = jnp.sum(got[:, :, 2 * ch :], axis=0)
    rows = got[:, :, 0 : 2 * ch]
    weighted = got[:, :, 2 * ch :]
    means = jnp.sum(rows * weighted, axis=0) / n_all
    dev = rows - means[None]
    spread = jnp.sum(dev * dev * weighted, axis=0)
    second = (jnp.sum(rows, axis=0) + pltpu.roll(spread, ch, axis=1)) / n_all
    mean_c, inv_c = columns(jnp.where(lane < ch, means, lax.rsqrt(second + EPS)))
    scale_c = pfn_gb[:, 0:1] * inv_c
    shift_c = scale_c * (m_loc - mean_c) + pfn_gb[:, 1:2]

    ids = lax.broadcasted_iota(jnp.int32, (1, pix), 1)
    col_id = ids & (w2 - 1)
    row_id = lax.shift_right_logical(ids, w2.bit_length() - 1) & (h2 - 1)

    def moved(x, dr, dc):
        ok = None
        if dc == -1:
            ok = col_id >= 1
        elif dc == 1:
            ok = col_id < w2 - 1
        if dr == -1:
            rok = row_id >= 1
            ok = rok if ok is None else ok & rok
        elif dr == 1:
            rok = row_id < h2 - 1
            ok = rok if ok is None else ok & rok
        if ok is None:
            return x
        return jnp.where(ok, pltpu.roll(x, (-(dr * w2 + dc)) % pix, axis=1), 0.0)

    planes = [[], [], [], []]
    for s in range(sweeps):
        pillar = jnp.maximum(jnp.max(mx[s], axis=1) * scale_c + shift_c, 0.0)
        hi, lo = split(pillar)
        placed = dot(jnp.concatenate([hi, lo], axis=0), onehot[s], NT)
        for k in range(4):
            part = placed[:, k * plane : (k + 1) * plane]
            planes[k].append(part[0:ch] + part[ch : 2 * ch])
    planes = [jnp.concatenate(p, axis=1) for p in planes]
    for a in range(3):
        for b in range(3):
            which = (0 if a == 1 else 2) + (0 if b == 1 else 1)
            tap = moved(planes[which], -1 if a == 0 else 0, -1 if b == 0 else 0)
            hi, lo = split(tap)
            at = pl.ds((3 * a + b) * ch, ch)
            xs[0, 0, at, :] = hi
            xs[0, 1, at, :] = lo

    entries_loc = float(pix)
    entries = float(pix * n)

    def fold(x):
        out = x[:, 0:128]
        for t in range(1, pix // 128):
            out = out + x[:, t * 128 : (t + 1) * 128]
        return out

    for layer in range(LAYERS):
        big = dot(wfs[layer], xs[layer, 0])
        z = big[0:ch] + big[ch : 2 * ch] + dot(wfs[layer, 0:ch, :], xs[layer, 1])
        sums = fold(z)
        m_loc = jnp.sum(sums, axis=1, keepdims=True) / entries_loc
        d = z - m_loc
        turned = jnp.concatenate([sums, fold(d * d)], axis=0).T
        row = jnp.sum(turned, axis=0, keepdims=True)
        row = jnp.where(lane < ch, row / entries_loc, row)
        send_row(st, layer + 1, row)
        rows = wait_row(st, layer + 1)
        total = jnp.sum(rows, axis=0)
        means = total / float(n)
        dev = rows - means[None]
        spread = jnp.sum(dev * dev, axis=0) * entries_loc
        second = (total + pltpu.roll(spread, ch, axis=1)) / entries
        row = jnp.where(lane < ch, means, lax.rsqrt(second + EPS))
        mean_c, inv_c = columns(row)
        normed = (z - mean_c) * inv_c
        y = bn_cols[:, layer : layer + 1] * normed
        y = y + bn_cols[:, LAYERS + layer : LAYERS + layer + 1]
        xh[layer] = normed
        yy[layer] = y
        sq[layer, :, :] = jnp.broadcast_to(row, (8, 2 * ch))
        act = y * jax.nn.sigmoid(y)
        if layer + 1 < LAYERS:
            for a in range(3):
                for b in range(3):
                    hi, lo = split(moved(act, a - 1, b - 1))
                    at = pl.ds((3 * a + b) * ch, ch)
                    xs[layer + 1, 0, at, :] = hi
                    xs[layer + 1, 1, at, :] = lo
        else:
            for s in range(sweeps):
                for r in range(h2):
                    at = s * plane + r * w2
                    feat[s, :, r, :] = act[:, at : at + w2]

    def weight_grad(layer):
        both = gz_s[...]
        big = dot(both, xs[layer, 0], NT)
        dw = big[0:ch] + big[ch : 2 * ch] + dot(both[0:ch], xs[layer, 1], NT)
        for j in range(owners):
            rs[layer, j] = dw[j * rows_per : (j + 1) * rows_per, :]
        send_parts(layer)

    u = jnp.concatenate([cot[s, :, r, :] for s in range(sweeps) for r in range(h2)], axis=1)
    for layer in range(LAYERS - 1, -1, -1):
        y = yy[layer]
        normed = xh[layer]
        sig = jax.nn.sigmoid(y)
        gy = u * (sig * (1.0 + y * (1.0 - sig)))
        turned = jnp.concatenate([fold(gy), fold(gy * normed)], axis=0).T
        rnd = 2 * LAYERS - layer
        send_row(st, rnd, jnp.sum(turned, axis=0, keepdims=True))
        if layer < LAYERS - 1:
            weight_grad(layer + 1)
        if layer < LAYERS - 2:
            add_parts(layer + 2)
        row = jnp.sum(wait_row(st, rnd), axis=0)
        norms[0, layer : layer + 1, :] = row[:, ch : 2 * ch]
        norms[1, layer : layer + 1, :] = row[:, 0:ch]
        dy_c, dyx_c = columns(row / entries)
        inv_c = columns(sq[layer, 0:1, :])[1]
        gz = (bn_cols[:, layer : layer + 1] * inv_c) * (gy - dy_c - normed * dyx_c)
        hi, lo = split(gz)
        gz_s[0:ch, :] = hi
        gz_s[ch : 2 * ch, :] = lo
        if layer > 0:
            for a in range(3):
                for b in range(3):
                    hi, lo = split(moved(gz, 1 - a, 1 - b))
                    at = pl.ds((3 * a + b) * ch, ch)
                    gs[0, at, :] = hi
                    gs[1, at, :] = lo
            big = dot(wbs[layer - 1], gs[0])
            u = big[0:ch] + big[ch : 2 * ch] + dot(wbs[layer - 1, 0:ch, :], gs[1])
    weight_grad(0)
    add_parts(1)
    for dr in range(2):
        for dc in range(2):
            hi, lo = split(moved(gz, dr, dc))
            at = pl.ds((2 * dr + dc) * ch, ch)
            gs[0, at, :] = hi
            gs[1, at, :] = lo
    big = dot(wb0s[...], gs[0, 0 : 4 * ch, :])
    u0 = big[0 : 4 * ch] + big[4 * ch :] + dot(wb0s[0 : 4 * ch, :], gs[1, 0 : 4 * ch, :])
    for s in range(sweeps):
        total = None
        for k in range(4):
            hi, lo = split(u0[k * ch : (k + 1) * ch, s * plane : (s + 1) * plane])
            part = dot(
                jnp.concatenate([hi, lo], axis=0), onehot[s, k * plane : (k + 1) * plane, :]
            )
            total = part if total is None else total + part
        pgrad[s] = total[0:ch] + total[ch : 2 * ch]
    add_parts(0)

    for layer in range(LAYERS):
        others = grads.at[layer, pl.ds(0, owners - 1)]
        if owners == n:
            pltpu.make_async_copy(others, others, ag_recv.at[layer]).wait()
        else:
            all_of = grads.at[layer]

            @pl.when(me < owners)
            def _():
                pltpu.make_async_copy(others, others, ag_recv.at[layer]).wait()

            @pl.when(me >= owners)
            def _():
                pltpu.make_async_copy(all_of, all_of, ag_recv.at[layer]).wait()

    for rnd in range(2 * LAYERS + 1):
        most = (st0.at[0] if rnd == 0 else st.at[rnd]).at[pl.ds(0, n - 1)]
        pltpu.make_async_copy(most, most, st_send.at[rnd]).wait()
    for layer in range(LAYERS):
        others = rs.at[layer, pl.ds(0, owners - 1)]
        sent = rbuf.at[layer, pl.ds(0, n - 1)]
        if owners == n:
            pltpu.make_async_copy(others, others, rs_send.at[layer]).wait()
            pltpu.make_async_copy(sent, sent, ag_send.at[layer]).wait()
        else:
            all_of = rs.at[layer]

            @pl.when(me < owners)
            def _():
                pltpu.make_async_copy(others, others, rs_send.at[layer]).wait()
                pltpu.make_async_copy(sent, sent, ag_send.at[layer]).wait()

            @pl.when(me >= owners)
            def _():
                pltpu.make_async_copy(all_of, all_of, rs_send.at[layer]).wait()


def per_device(
    n_rack,
    n_chip,
    points,
    counts,
    cells,
    pfn_weight,
    pfn_gain,
    pfn_bias,
    conv_weight,
    bn_gain,
    bn_bias,
    cotangent,
):
    sweeps, _, maxp, pill = points.shape
    ch = pfn_weight.shape[1]
    h2, w2 = cotangent.shape[2:]
    gh, gw = 2 * h2, 2 * w2
    n = n_rack * n_chip
    owners = min(n, ch)
    rows_per = ch // owners
    pix = sweeps * h2 * w2
    kdim = 9 * ch
    taps = conv_weight.reshape(LAYERS, 9, ch, ch)
    wf = taps.transpose(0, 2, 1, 3).reshape(LAYERS, ch, kdim)
    wb = taps[1:].transpose(0, 3, 1, 2).reshape(LAYERS - 1, ch, kdim)
    first = taps[0].transpose(0, 2, 1)
    zero = jnp.zeros((ch, ch), F32)
    tap_of = {(0, 0): 1, (1, 0): 2, (1, 1): 0}
    blocks = []
    for row_par in range(2):
        for col_par in range(2):
            line = []
            for dr in range(2):
                for dc in range(2):
                    a, b = tap_of.get((row_par, dr)), tap_of.get((col_par, dc))
                    line.append(zero if a is None or b is None else first[3 * a + b])
            blocks.append(line)
    wb0 = jnp.block(blocks)
    dims = (n_rack, n_chip, sweeps, maxp, gh, gw, pill, ch, owners)
    vmem = pl.BlockSpec(memory_space=pltpu.VMEM)
    smem = pl.BlockSpec(memory_space=pltpu.SMEM)
    feat, grads, norms, pgrad = pl.pallas_call(
        functools.partial(kernel, dims),
        out_shape=(
            jax.ShapeDtypeStruct((sweeps, ch, h2, w2), F32),
            jax.ShapeDtypeStruct((LAYERS, owners, rows_per, kdim), F32),
            jax.ShapeDtypeStruct((2, LAYERS, ch), F32),
            jax.ShapeDtypeStruct((sweeps, ch, pill), F32),
        ),
        in_specs=[vmem, vmem, vmem, smem] + [vmem] * 7,
        out_specs=(vmem, vmem, vmem, vmem),
        scratch_shapes=[
            pltpu.VMEM((LAYERS, 2, kdim, pix), BF16),
            pltpu.VMEM((2, kdim, pix), BF16),
            pltpu.VMEM((LAYERS, 2 * ch, kdim), BF16),
            pltpu.VMEM((LAYERS - 1, 2 * ch, kdim), BF16),
            pltpu.VMEM((8 * ch, 4 * ch), BF16),
            pltpu.VMEM((sweeps, gh * gw, pill), BF16),
            pltpu.VMEM((sweeps, ch, pill), F32),
            pltpu.VMEM((sweeps, ch, 8, pill), F32),
            pltpu.VMEM((ch, 8, 128), F32),
            pltpu.VMEM((LAYERS, ch, pix), F32),
            pltpu.VMEM((LAYERS, ch, pix), F32),
            pltpu.VMEM((2 * ch, pix), BF16),
            pltpu.VMEM((1, n, 1, 4 * ch), F32),
            pltpu.VMEM((2 * LAYERS + 1, n, 1, 2 * ch), F32),
            pltpu.VMEM((LAYERS, owners, rows_per, kdim), F32),
            pltpu.VMEM((LAYERS, n, rows_per, kdim), F32),
            pltpu.SemaphoreType.DMA((2 * LAYERS + 1,)),
            pltpu.SemaphoreType.DMA((2 * LAYERS + 1,)),
            pltpu.SemaphoreType.DMA((LAYERS,)),
            pltpu.SemaphoreType.DMA((LAYERS,)),
            pltpu.SemaphoreType.DMA((LAYERS,)),
            pltpu.SemaphoreType.DMA((LAYERS,)),
        ],
        compiler_params=pltpu.CompilerParams(
            collective_id=0, has_side_effects=True, vmem_limit_bytes=60 * 1024 * 1024
        ),
    )(
        points,
        counts,
        cells,
        pfn_weight,
        pfn_weight.T,
        jnp.stack([pfn_gain, pfn_bias], axis=1),
        wf,
        wb,
        wb0,
        jnp.concatenate([bn_gain, bn_bias], axis=0).T,
        cotangent,
    )
    grads = grads.reshape(LAYERS, ch, 9, ch).transpose(0, 2, 1, 3)
    return (feat, grads.reshape(LAYERS, 9, ch * ch), norms, pgrad)


def solution(mesh):
    both = ("rack", "chip")
    return jax.shard_map(
        functools.partial(per_device, mesh.shape["rack"], mesh.shape["chip"]),
        mesh=mesh,
        in_specs=(
            P(both, None, None, None),
            P(both, None),
            P(both, None),
            P(),
            P(),
            P(),
            P(),
            P(),
            P(),
            P(both, None, None, None),
        ),
        out_specs=(
            P(both, None, None, None),
            P(),
            P(),
            P(both, None, None),
        ),
        check_vma=False,
    )
```

profile of v0, /device:TPU:0, one launch (start us, length us, event | category | flops | bytes accessed | tf_op | source)
XLA Modules:
  0.0 99.1 jit_solution(10240626361280117460)
XLA Ops:
  0.6 0.7 pad_maximum_fusion.1
  1.3 0.7 pad_maximum_fusion
  2.0 0.7 copy.47
  2.7 0.7 copy.48.pfn_gb
  3.4 1.4 %copy.43 = f32[9,64]{0,1:T(8,128)} copy(f32[9,64]{1,0:T(8,128)} %pw_s.1) | data formatting | bytes 4608 | tf_op args[3]
  4.8 1.4 %slice_reduce_fusion = f32[9,4096]{1,0:T(8,128)S(1)} fusion(f32[4,9,4096]{2,0,1:T(4,128)} %param.16), kind=kLoop, calls=%fused_computation.1 | loop fusion | bytes 294912 | tf_op jit(solution)/shard_map/slice | solution.py:469
  6.3 0.0 copy-start
  6.3 0.1 squeeze.30
  6.4 0.1 copy.46
  6.6 0.9 maximum_maximum_fusion.wb0
  7.4 0.0 copy-done
  7.4 0.2 slice.37
  7.6 0.5 slice.38
  8.1 0.1 copy.45
  8.2 1.1 %copy.50.wb = f32[3,64,576]{2,1,0:T(8,128)} copy(f32[3,64,576]{1,2,0:T(8,128)S(1)} %bitcast.40) | data formatting | bytes 884736 | tf_op jit(solution)/shard_map/reshape | solution.py:468
  9.3 0.6 reshape.26
  9.8 0.4 copy.44
  10.2 1.2 %copy.49.wf = f32[4,64,576]{2,1,0:T(8,128)} copy(f32[4,64,576]{1,2,0:T(8,128)S(1)} %bitcast.39) | data formatting | bytes 1179648 | tf_op jit(solution)/shard_map/reshape | solution.py:467
  11.4 82.2 %shard_map.129 = (f32[2,64,4,128]{3,2,1,0:T(4,128)}, f32[4,32,2,576]{3,2,1,0:T(2,128)}, f32[2,4,64]{2,1,0:T(4,128)}, f32[2,64,256]{2,1,0:T(8,128)}) custom-call(f32[2,4,32,256]{3,2,1,0:T(8,128)} %points.1, s32[2,256]{1,0:T(2,128)} %counts.1, s32[2,256]{1,0:T(2,128)} %cells.1, f32[9,64]{1,0:T(8,128)} %pw_s.1, f32[64,9]{1,0:T(8,128)} %bitcast.42, ...), custom_call_target="tpu_custom_call" | custom-call | tf_op jit(solution)/shard_map/pallas_call | solution.py:485
  93.7 1.8 %reshape.29 = f32[4,64,9,64]{3,2,1,0:T(8,128)S(1)} reshape(f32[4,32,2,576]{3,2,1,0:T(2,128)} %get-tuple-element.9) | data formatting | bytes 1179648 | tf_op jit(solution)/shard_map/reshape | solution.py:535
  95.4 0.4 copy.51
  95.8 0.0 copy-start.1
  95.8 0.0 copy-start.3
  95.8 0.0 copy-start.2
  95.8 1.3 %reshape.30 = f32[4,9,4096]{2,0,1:T(4,128)} reshape(f32[4,9,64,64]{3,2,0,1:T(8,128)S(1)} %copy.51) | data formatting | bytes 1179648 | tf_op jit(solution)/shard_map/reshape | solution.py:536
  97.2 0.0 copy-done.1
  97.2 0.7 copy.55
  97.9 0.0 copy-done.3
  97.9 0.6 copy.56
  98.5 0.0 copy-done.2
  98.5 0.7 copy.57
  (2 shorter events, 0.0 us)
Async XLA Ops:
  6.3 1.2 %copy-start = (f32[4,9,4096]{2,0,1:T(4,128)S(1)}, f32[4,9,4096]{2,0,1:T(4,128)}, u32[]{:S(2)}) copy-start(f32[4,9,4096]{2,0,1:T(4,128)} %param.16) | copy-start | bytes 1769476
  95.8 1.3 %copy-start.1 = (f32[2,64,4,128]{3,2,1,0:T(4,128)S(1)}, f32[2,64,4,128]{3,2,1,0:T(4,128)}, u32[]{:S(2)}) copy-start(f32[2,64,4,128]{3,2,1,0:T(4,128)} %get-tuple-element.25) | copy-start | bytes 786436
  95.8 2.0 %copy-start.3 = (f32[2,4,64]{2,1,0:T(4,128)S(1)}, f32[2,4,64]{2,1,0:T(4,128)}, u32[]{:S(2)}) copy-start(f32[2,4,64]{2,1,0:T(4,128)} %get-tuple-element.27) | copy-start | bytes 6148
  95.8 2.6 %copy-start.2 = (f32[2,64,256]{2,1,0:T(8,128)S(1)}, f32[2,64,256]{2,1,0:T(8,128)}, u32[]{:S(2)}) copy-start(f32[2,64,256]{2,1,0:T(8,128)} %get-tuple-element.28) | copy-start | bytes 393220
where the time goes:
time: 99.4 us; the launch traced here: 99.1 us
  Pallas kernels  82.2 us (83%)
  local copies, waits for them, and re-layouts  13.9 us (14%)
  other arithmetic  2.26 us (2%)
    pallas_call x1, Pallas kernels, per_device(): pl.pallas_call(functools.partial(kernel, dims), out_shape=(jax.ShapeDtype...  82.2 us
    unnamed x12, local copies, waits for them, and re-layouts  3.37 us

commit v1 on v0

--- a/solution.py
+++ b/solution.py
@@ -16,6 +16,11 @@
 LOWEST = -3e38
 
 
+class Peer:
+    def __init__(self, rack, chip, index):
+        self.rack, self.chip, self.index = rack, chip, index
+
+
 def dot(a, b, dims=NN):
     return lax.dot_general(a, b, dims, preferred_element_type=F32)
 
@@ -32,15 +37,15 @@
     counts,
     cells,
     pw_s,
-    pw_t,
-    pfn_gb,
-    wf,
-    wb,
-    wb0,
-    bn_cols,
+    pw,
+    pfn_gain,
+    pfn_bias,
+    w4,
+    bn_gain,
+    bn_bias,
     cot,
     feat,
-    grads,
+    out_g,
     norms,
     pgrad,
     xs,
@@ -49,6 +54,9 @@
     wbs,
     wb0s,
     onehot,
+    par,
+    cot_s,
+    grads,
     bm,
     mx,
     sq,
@@ -73,12 +81,27 @@
     pix = sweeps * plane
     rows_per = ch // owners
     kdim = 9 * ch
-    me = lax.axis_index("rack") * n_chip + lax.axis_index("chip")
+    my_rack, my_chip = lax.axis_index("rack"), lax.axis_index("chip")
+    me = my_rack * n_chip + my_chip
 
     def device(t):
+        if isinstance(t, Peer):
+            return {"rack": t.rack, "chip": t.chip}
         return {"rack": lax.div(t, n_chip), "chip": lax.rem(t, n_chip)}
 
+    def far(k):
+        dr, dc = divmod(k, n_chip)
+        return -min(dc, n_chip - dc) - min(dr, n_rack - dr)
+
     def peers(body):
+        if n <= 32:
+            for k in sorted(range(1, n), key=far):
+                dr, dc = divmod(k, n_chip)
+                rack = lax.rem(my_rack + dr, n_rack) if dr else my_rack
+                chip = lax.rem(my_chip + dc, n_chip) if dc else my_chip
+                body(Peer(rack, chip, rack * n_chip + chip))
+            return
+
         def step(k, carry):
             body(lax.rem(me + k, n))
             return carry
@@ -116,7 +139,7 @@
         def go(t):
             def copy():
                 pltpu.make_async_remote_copy(
-                    src_ref=rs.at[layer, t],
+                    src_ref=rs.at[layer, t.index if isinstance(t, Peer) else t],
                     dst_ref=rbuf.at[layer, me],
                     send_sem=rs_send.at[layer],
                     recv_sem=rs_recv.at[layer],
@@ -161,6 +184,7 @@
     slot = lax.broadcasted_iota(jnp.int32, (maxp, pill), 0)
     lane = lax.broadcasted_iota(jnp.int32, (1, 2 * ch), 1)
     per_sweep = []
+    spots = []
     totals = [jnp.zeros((1, 1), F32)] * 9
     n_loc = jnp.zeros((1, 1), F32)
     for s in range(sweeps):
@@ -181,10 +205,17 @@
         per_sweep.append(cents + [col_pos, row_pos])
         spot = ((row & 1) * 2 + (col & 1)) * plane
         spot = spot + lax.shift_right_logical(row, 1) * w2 + lax.shift_right_logical(col, 1)
-        for k in range(4):
-            ids = lax.broadcasted_iota(jnp.int32, (plane, pill), 0) + k * plane
-            onehot[s, k * plane : (k + 1) * plane, :] = (ids == spot).astype(F32).astype(BF16)
-    pw_cols = pw_t[...]
+        spots.append(spot)
+    par[...] = jnp.zeros(par.shape, F32)
+    par[0:9, 0:ch] = pw[...]
+    par[9:10, 0:ch] = pfn_gain[...]
+    par[10:11, 0:ch] = pfn_bias[...]
+    par[11 : 11 + LAYERS, 0:ch] = bn_gain[...]
+    par[11 + LAYERS : 11 + 2 * LAYERS, 0:ch] = bn_bias[...]
+    par_cols = par[...].T
+    pw_cols = par_cols[0:ch, 0:9]
+    gain_c, bias_c = par_cols[0:ch, 9:10], par_cols[0:ch, 10:11]
+    bn_cols = par_cols[0:ch, 11 : 11 + 2 * LAYERS]
     m_loc = jnp.zeros((ch, 1), F32)
     for f in range(9):
         m_loc = m_loc + pw_cols[:, f : f + 1] * totals[f]
@@ -230,17 +261,38 @@
     pl.semaphore_wait(barrier, n - 1)
     send_row(st0, 0, row)
 
-    for layer in range(LAYERS):
-        hi, lo = split(wf[layer])
+    def forward_weights(layer):
+        w = [w4[layer, t * ch : (t + 1) * ch, :] for t in range(9)]
+        hi, lo = split(jnp.concatenate(w, axis=1))
         wfs[layer, 0:ch, :] = hi
         wfs[layer, ch : 2 * ch, :] = lo
-    for layer in range(LAYERS - 1):
-        hi, lo = split(wb[layer])
-        wbs[layer, 0:ch, :] = hi
-        wbs[layer, ch : 2 * ch, :] = lo
-    hi, lo = split(wb0[...])
-    wb0s[0 : 4 * ch, :] = hi
-    wb0s[4 * ch : 8 * ch, :] = lo
+
+    def backward_weights(layer):
+        hi, lo = split(w4[layer].T)
+        wbs[layer - 1, 0:ch, :] = hi
+        wbs[layer - 1, ch : 2 * ch, :] = lo
+
+    def first_backward_weights():
+        w = w4[0].T
+        zero = jnp.zeros((ch, ch), F32)
+        tap_of = {(0, 0): 1, (1, 0): 2, (1, 1): 0}
+        for k in range(4):
+            line = []
+            for j in range(4):
+                a, b = tap_of.get((k // 2, j // 2)), tap_of.get((k % 2, j % 2))
+                t = None if a is None or b is None else 3 * a + b
+                line.append(zero if t is None else w[:, t * ch : (t + 1) * ch])
+            hi, lo = split(jnp.concatenate(line, axis=1))
+            wb0s[k * ch : (k + 1) * ch, :] = hi
+            wb0s[(4 + k) * ch : (5 + k) * ch, :] = lo
+
+    for s in range(sweeps):
+        for k in range(4):
+            ids = lax.broadcasted_iota(jnp.int32, (plane, pill), 0) + k * plane
+            onehot[s, k * plane : (k + 1) * plane, :] = (ids == spots[s]).astype(F32).astype(BF16)
+    for s in range(sweeps):
+        bm[s] = jnp.max(mx[s], axis=1)
+    forward_weights(0)
 
     def columns(row):
         turned = jnp.broadcast_to(row, (8, 2 * ch)).T
@@ -255,8 +307,8 @@
     spread = jnp.sum(dev * dev * weighted, axis=0)
     second = (jnp.sum(rows, axis=0) + pltpu.roll(spread, ch, axis=1)) / n_all
     mean_c, inv_c = columns(jnp.where(lane < ch, means, lax.rsqrt(second + EPS)))
-    scale_c = pfn_gb[:, 0:1] * inv_c
-    shift_c = scale_c * (m_loc - mean_c) + pfn_gb[:, 1:2]
+    scale_c = gain_c * inv_c
+    shift_c = scale_c * (m_loc - mean_c) + bias_c
 
     ids = lax.broadcasted_iota(jnp.int32, (1, pix), 1)
     col_id = ids & (w2 - 1)
@@ -280,7 +332,7 @@
 
     planes = [[], [], [], []]
     for s in range(sweeps):
-        pillar = jnp.maximum(jnp.max(mx[s], axis=1) * scale_c + shift_c, 0.0)
+        pillar = jnp.maximum(bm[s] * scale_c + shift_c, 0.0)
         hi, lo = split(pillar)
         placed = dot(jnp.concatenate([hi, lo], axis=0), onehot[s], NT)
         for k in range(4):
@@ -305,6 +357,10 @@
             out = out + x[:, t * 128 : (t + 1) * 128]
         return out
 
+    def slope(y):
+        sig = jax.nn.sigmoid(y)
+        return sig * (1.0 + y * (1.0 - sig))
+
     for layer in range(LAYERS):
         big = dot(wfs[layer], xs[layer, 0])
         z = big[0:ch] + big[ch : 2 * ch] + dot(wfs[layer, 0:ch, :], xs[layer, 1])
@@ -315,6 +371,18 @@
         row = jnp.sum(turned, axis=0, keepdims=True)
         row = jnp.where(lane < ch, row / entries_loc, row)
         send_row(st, layer + 1, row)
+        if layer == 0:
+            first_backward_weights()
+        else:
+            backward_weights(layer)
+            yy[layer - 1] = slope(yy[layer - 1])
+        if layer + 1 < LAYERS:
+            forward_weights(layer + 1)
+        else:
+            for s in range(sweeps):
+                for r in range(h2):
+                    at = s * plane + r * w2
+                    cot_s[:, at : at + w2] = cot[s, :, r, :]
         rows = wait_row(st, layer + 1)
         total = jnp.sum(rows, axis=0)
         means = total / float(n)
@@ -327,9 +395,10 @@
         y = bn_cols[:, layer : layer + 1] * normed
         y = y + bn_cols[:, LAYERS + layer : LAYERS + layer + 1]
         xh[layer] = normed
-        yy[layer] = y
         sq[layer, :, :] = jnp.broadcast_to(row, (8, 2 * ch))
-        act = y * jax.nn.sigmoid(y)
+        sig = jax.nn.sigmoid(y)
+        act = y * sig
+        yy[layer] = y if layer + 1 < LAYERS else sig * (1.0 + y * (1.0 - sig))
         if layer + 1 < LAYERS:
             for a in range(3):
                 for b in range(3):
@@ -337,11 +406,6 @@
                     at = pl.ds((3 * a + b) * ch, ch)
                     xs[layer + 1, 0, at, :] = hi
                     xs[layer + 1, 1, at, :] = lo
-        else:
-            for s in range(sweeps):
-                for r in range(h2):
-                    at = s * plane + r * w2
-                    feat[s, :, r, :] = act[:, at : at + w2]
 
     def weight_grad(layer):
         both = gz_s[...]
@@ -351,15 +415,18 @@
             rs[layer, j] = dw[j * rows_per : (j + 1) * rows_per, :]
         send_parts(layer)
 
-    u = jnp.concatenate([cot[s, :, r, :] for s in range(sweeps) for r in range(h2)], axis=1)
+    u = cot_s[...]
     for layer in range(LAYERS - 1, -1, -1):
-        y = yy[layer]
         normed = xh[layer]
-        sig = jax.nn.sigmoid(y)
-        gy = u * (sig * (1.0 + y * (1.0 - sig)))
+        gy = u * yy[layer]
         turned = jnp.concatenate([fold(gy), fold(gy * normed)], axis=0).T
         rnd = 2 * LAYERS - layer
         send_row(st, rnd, jnp.sum(turned, axis=0, keepdims=True))
+        if layer == LAYERS - 1:
+            for s in range(sweeps):
+                for r in range(h2):
+                    at = s * plane + r * w2
+                    feat[s, :, r, :] = act[:, at : at + w2]
         if layer < LAYERS - 1:
             weight_grad(layer + 1)
         if layer < LAYERS - 2:
@@ -403,7 +470,7 @@
         pgrad[s] = total[0:ch] + total[ch : 2 * ch]
     add_parts(0)
 
-    for layer in range(LAYERS):
+    for layer in range(LAYERS - 1, -1, -1):
         others = grads.at[layer, pl.ds(0, owners - 1)]
         if owners == n:
             pltpu.make_async_copy(others, others, ag_recv.at[layer]).wait()
@@ -417,6 +484,10 @@
             @pl.when(me >= owners)
             def _():
                 pltpu.make_async_copy(all_of, all_of, ag_recv.at[layer]).wait()
+
+        whole = grads[layer].reshape(ch, kdim)
+        for t in range(9):
+            out_g[layer, t] = whole[:, t * ch : (t + 1) * ch]
 
     for rnd in range(2 * LAYERS + 1):
         most = (st0.at[0] if rnd == 0 else st.at[rnd]).at[pl.ds(0, n - 1)]
@@ -463,30 +534,14 @@
     rows_per = ch // owners
     pix = sweeps * h2 * w2
     kdim = 9 * ch
-    taps = conv_weight.reshape(LAYERS, 9, ch, ch)
-    wf = taps.transpose(0, 2, 1, 3).reshape(LAYERS, ch, kdim)
-    wb = taps[1:].transpose(0, 3, 1, 2).reshape(LAYERS - 1, ch, kdim)
-    first = taps[0].transpose(0, 2, 1)
-    zero = jnp.zeros((ch, ch), F32)
-    tap_of = {(0, 0): 1, (1, 0): 2, (1, 1): 0}
-    blocks = []
-    for row_par in range(2):
-        for col_par in range(2):
-            line = []
-            for dr in range(2):
-                for dc in range(2):
-                    a, b = tap_of.get((row_par, dr)), tap_of.get((col_par, dc))
-                    line.append(zero if a is None or b is None else first[3 * a + b])
-            blocks.append(line)
-    wb0 = jnp.block(blocks)
     dims = (n_rack, n_chip, sweeps, maxp, gh, gw, pill, ch, owners)
     vmem = pl.BlockSpec(memory_space=pltpu.VMEM)
     smem = pl.BlockSpec(memory_space=pltpu.SMEM)
-    feat, grads, norms, pgrad = pl.pallas_call(
+    feat, out_g, norms, pgrad = pl.pallas_call(
         functools.partial(kernel, dims),
         out_shape=(
             jax.ShapeDtypeStruct((sweeps, ch, h2, w2), F32),
-            jax.ShapeDtypeStruct((LAYERS, owners, rows_per, kdim), F32),
+            jax.ShapeDtypeStruct((LAYERS, 9, ch, ch), F32),
             jax.ShapeDtypeStruct((2, LAYERS, ch), F32),
             jax.ShapeDtypeStruct((sweeps, ch, pill), F32),
         ),
@@ -499,6 +554,9 @@
             pltpu.VMEM((LAYERS - 1, 2 * ch, kdim), BF16),
             pltpu.VMEM((8 * ch, 4 * ch), BF16),
             pltpu.VMEM((sweeps, gh * gw, pill), BF16),
+            pltpu.VMEM((32, 128), F32),
+            pltpu.VMEM((ch, pix), F32),
+            pltpu.VMEM((LAYERS, owners, rows_per, kdim), F32),
             pltpu.VMEM((sweeps, ch, pill), F32),
             pltpu.VMEM((sweeps, ch, 8, pill), F32),
             pltpu.VMEM((ch, 8, 128), F32),
@@ -524,16 +582,15 @@
         counts,
         cells,
         pfn_weight,
-        pfn_weight.T,
-        jnp.stack([pfn_gain, pfn_bias], axis=1),
-        wf,
-        wb,
-        wb0,
-        jnp.concatenate([bn_gain, bn_bias], axis=0).T,
+        pfn_weight,
+        pfn_gain.reshape(1, ch),
+        pfn_bias.reshape(1, ch),
+        conv_weight.reshape(LAYERS, kdim, ch),
+        bn_gain,
+        bn_bias,
         cotangent,
     )
-    grads = grads.reshape(LAYERS, ch, 9, ch).transpose(0, 2, 1, 3)
-    return (feat, grads.reshape(LAYERS, 9, ch * ch), norms, pgrad)
+    return (feat, out_g.reshape(LAYERS, 9, ch * ch), norms, pgrad)
 
 
 def solution(mesh):

time: 99.4 us -> 87.8 us (0.88)
  local copies, waits for them, and re-layouts: 13.9 us -> 7.77 us
  Pallas kernels: 82.2 us -> 79.1 us
  other arithmetic: 2.26 us -> 0 us
    pallas_call x1, Pallas kernels: 82.2 us -> 79.1 us  [per_device(): pl.pallas_call(functools.partial(kernel, dims), out_shape=(jax.ShapeDtype...]
    slice x4 -> x0, local copies, waits for them, and re-layouts: 2.16 us -> none  [the longest x1 1.45 us: per_device(): first = taps[0].transpose(0, 2, 1)]
    reshape x6 -> x3, local copies, waits for them, and re-layouts: 6.35 us -> 4.38 us  [the longest x2 2.89 us: per_device(): return (feat, out_g.reshape(LAYERS, 9, ch * ch), norms, pgrad)]
    concatenate x2 -> x0, other arithmetic: 1.58 us -> none  [the longest x1 0.88 us: per_device(): wb0 = jnp.block(blocks)]
    unnamed x12 -> x10, local copies, waits for them, and re-layouts: 3.37 us -> 3.39 us
where the time goes in v1:
time: 87.8 us; the launch traced here: 87.5 us
  Pallas kernels  79.1 us (90%)
  local copies, waits for them, and re-layouts  7.77 us (9%)
    pallas_call x1, Pallas kernels, per_device(): pl.pallas_call(functools.partial(kernel, dims), out_shape=(jax.ShapeDtype...  79.1 us
    unnamed x10, local copies, waits for them, and re-layouts  3.39 us
    reshape x2, local copies, waits for them, and re-layouts, per_device(): return (feat, out_g.reshape(LAYERS, 9, ch * ch), norms, pgrad)  2.89 us

profile of v1, /device:TPU:0, one launch (start us, length us, event | category | flops | bytes accessed | tf_op | source)
XLA Modules:
  0.0 87.5 jit_solution(12281726996186627643)
XLA Ops:
  0.6 1.4 %copy.16 = f32[4,9,4096]{2,1,0:T(8,128)S(1)} copy(f32[4,9,4096]{2,0,1:T(4,128)} %param.16) | data formatting | bytes 1179648 | tf_op args[6]
  2.1 1.5 %reshape.22.w4 = f32[4,576,64]{2,1,0:T(8,128)} reshape(f32[4,9,4096]{2,1,0:T(8,128)S(1)} %copy.16) | data formatting | bytes 1179648 | tf_op jit(solution)/shard_map/reshape | solution.py:588
  3.5 79.1 %shard_map.129 = (f32[2,64,4,128]{3,2,1,0:T(4,128)}, f32[4,9,64,64]{3,2,1,0:T(8,128)}, f32[2,4,64]{2,1,0:T(4,128)}, f32[2,64,256]{2,1,0:T(8,128)}) custom-call(f32[2,4,32,256]{3,2,1,0:T(8,128)} %points.1, s32[2,256]{1,0:T(2,128)} %counts.1, s32[2,256]{1,0:T(2,128)} %cells.1, f32[9,64]{1,0:T(8,128)} %pw.1, f32[9,64]{1,0:T(8,128)} %pw.1, f32[1,64]{1,0:T(1,128)} %bitcast.4, ...), custom_call_target="tpu_custom_call" | custom-call | tf_op jit(solution)/shard_map/pallas_call | solution.py:540
  82.7 1.7 %reshape.24 = f32[4,9,4096]{2,1,0:T(8,128)S(1)} reshape(f32[4,9,64,64]{3,2,1,0:T(8,128)} %get-tuple-element.9) | data formatting | bytes 1179648 | tf_op jit(solution)/shard_map/reshape | solution.py:593
  84.4 0.0 copy-start
  84.4 0.0 copy-start.2
  84.4 0.0 copy-start.1
  84.4 1.2 %copy.18 = f32[4,9,4096]{2,0,1:T(4,128)} copy(f32[4,9,4096]{2,1,0:T(8,128)S(1)} %reshape.24) | data formatting | bytes 1179648 | tf_op jit(solution)/shard_map/reshape | solution.py:593
  85.6 0.0 copy-done
  85.6 0.7 copy.22
  86.3 0.0 copy-done.2
  86.3 0.6 copy.23
  86.9 0.0 copy-done.1
  86.9 0.7 copy.24
Async XLA Ops:
  84.4 1.2 %copy-start = (f32[2,64,4,128]{3,2,1,0:T(4,128)S(1)}, f32[2,64,4,128]{3,2,1,0:T(4,128)}, u32[]{:S(2)}) copy-start(f32[2,64,4,128]{3,2,1,0:T(4,128)} %get-tuple-element.20) | copy-start | bytes 786436
  84.4 1.9 %copy-start.2 = (f32[2,4,64]{2,1,0:T(4,128)S(1)}, f32[2,4,64]{2,1,0:T(4,128)}, u32[]{:S(2)}) copy-start(f32[2,4,64]{2,1,0:T(4,128)} %get-tuple-element.22) | copy-start | bytes 6148
  84.4 2.5 %copy-start.1 = (f32[2,64,256]{2,1,0:T(8,128)S(1)}, f32[2,64,256]{2,1,0:T(8,128)}, u32[]{:S(2)}) copy-start(f32[2,64,256]{2,1,0:T(8,128)} %get-tuple-element.23) | copy-start | bytes 393220
